TPU v7x, 32 devices: a whole 2x2x4 slice. The times are simulated.
32 devices in a mesh: dp: 4 (over x, core), tensor: 8 (over z, y).
Axes of the slice: x: 2, y: 2, z: 4, core: 2. Of those that a mesh axis runs over, the one named last changes fastest.
Arguments:
- out_grad: bfloat16 [2, 320, 4096], P(None, 'dp', 'tensor'), may hold values from -0.3125 to 0.3125
- layer_input: bfloat16 [2, 320, 4096], P(None, 'dp', 'tensor'), may hold values from -8 to 8
- w_down: bfloat16 [16384, 4096], P('tensor'), may hold values from -0.046875 to 0.046875
- silu_gate: bfloat16 [2, 320, 16384], P(None, 'dp', 'tensor'), may hold values from -6 to 6
- up_proj: bfloat16 [2, 320, 16384], P(None, 'dp', 'tensor'), may hold values from -6 to 6
- slope_codes: int32 [2, 32, 16384], P(None, 'dp', 'tensor'), may hold values from 0 to 1073741823
Outputs:
- grad_down: bfloat16 [16384, 4096], P('tensor', 'dp')
- grad_gate: bfloat16 [4096, 16384], P('dp', 'tensor')
- grad_up: bfloat16 [4096, 16384], P('dp', 'tensor')
Inputs may be any that keep to these rules, and one draw needn't show every extreme that they name: `slope_codes`: every word holds ten independent 3-bit codes; all eight codes occur.
All inputs are finite; a program needn't handle non-finite values.
Results may differ from a plain program's by a relative error of at most 0.018.
Values may be sent and summed in bfloat16 or wider, within the bound.
A program may use at most 128 MiB of HBM per device.

v0:
```python
import jax
import jax.numpy as jnp
from jax import lax
from jax.sharding import PartitionSpec as P

SLOPE_LEVELS = (-0.09, 0.06, 0.22, 0.41, 0.6, 0.79, 0.96, 1.08)


def decode_slopes(packed):
    shifts = 3 * jnp.arange(10, dtype=jnp.int32)
    pieces = jnp.bitwise_and(jnp.right_shift(packed[..., None, :], shifts[:, None]), 7)
    pieces = pieces.reshape(packed.shape[:-2] + (packed.shape[-2] * 10, packed.shape[-1]))
    result = jnp.full(pieces.shape, SLOPE_LEVELS[0], jnp.float32)
    for symbol in range(1, 8):
        result = jnp.where(pieces == symbol, jnp.float32(SLOPE_LEVELS[symbol]), result)
    return result


def shards(out_grad, layer_input, w_down, silu_gate, up_proj, slope_codes):
    micro_count = out_grad.shape[0]
    model_width = w_down.shape[1]
    hidden_width = w_down.shape[0]
    group_rows = micro_count * out_grad.shape[1]
    grad_rows, input_rows = (
        lax.all_gather(out_grad, "tensor", axis=2, tiled=True),
        lax.all_gather(layer_input, "tensor", axis=2, tiled=True),
    )
    output_all = grad_rows.reshape(-1, model_width)
    input_all = input_rows.reshape(-1, model_width)
    gate_act = silu_gate.reshape(-1, hidden_width).astype(jnp.float32)
    up_value = up_proj.reshape(-1, hidden_width).astype(jnp.float32)
    hidden = (gate_act * up_value).astype(jnp.bfloat16)
    slopes = decode_slopes(slope_codes).reshape(-1, hidden_width)
    hidden_grad = lax.dot_general(
        output_all, w_down, (((1,), (1,)), ((), ())), preferred_element_type=jnp.float32
    )
    up_grad = (hidden_grad * gate_act).astype(jnp.bfloat16)
    gate_grad = (hidden_grad * up_value * slopes).astype(jnp.bfloat16)
    block_inputs, block_outputs = (
        lax.all_to_all(input_all, "dp", split_axis=1, concat_axis=0, tiled=True),
        lax.all_to_all(output_all, "dp", split_axis=1, concat_axis=0, tiled=True),
    )
    activations = jnp.concatenate((gate_grad, up_grad, hidden), axis=1)
    values = lax.all_gather(activations, "dp", axis=0, tiled=True)
    row_count = values.shape[0]
    groups = row_count // group_rows
    inputs_3d = block_inputs.reshape(groups, group_rows, block_inputs.shape[1])
    outputs_3d = block_outputs.reshape(groups, group_rows, block_outputs.shape[1])
    values_3d = values.reshape(groups, group_rows, values.shape[1])
    gate_up_parts = jnp.einsum(
        "grd,grf->gdf",
        inputs_3d,
        values_3d[:, :, : 2 * hidden_width],
        preferred_element_type=jnp.float32,
    )
    down_parts = jnp.einsum(
        "grf,grd->gfd",
        values_3d[:, :, 2 * hidden_width :],
        outputs_3d,
        preferred_element_type=jnp.float32,
    )
    gate_up_sum = jnp.sum(gate_up_parts.astype(jnp.bfloat16).astype(jnp.float32), axis=0)
    down_sum = jnp.sum(down_parts.astype(jnp.bfloat16).astype(jnp.float32), axis=0)
    grad_down = down_sum.astype(jnp.bfloat16)
    grad_gate = gate_up_sum[:, :hidden_width].astype(jnp.bfloat16)
    grad_up = gate_up_sum[:, hidden_width:].astype(jnp.bfloat16)
    return (grad_down, grad_gate, grad_up)


def solution(mesh):
    return jax.shard_map(
        shards,
        mesh=mesh,
        in_specs=(
            P(None, "dp", "tensor"),
            P(None, "dp", "tensor"),
            P("tensor", None),
            P(None, "dp", "tensor"),
            P(None, "dp", "tensor"),
            P(None, "dp", "tensor"),
        ),
        out_specs=(P("tensor", "dp"), P("dp", "tensor"), P("dp", "tensor")),
        check_vma=False,
    )
```

profile of v0, /device:TPU:0, one launch (start us, length us, event | category | flops | bytes accessed | tf_op | source)
XLA Modules:
  0.0 234.2 jit_solution(13841438188736707465)
XLA Ops:
  7.2 0.0 all-gather.4.cloned.1.call-start
  7.2 0.7 all-gather.4.cloned.1.call-update
  7.9 0.0 all-gather.8.cloned.1.call-start
  7.9 0.7 all-gather.8.cloned.1.call-update
  8.6 0.0 all-gather.6.cloned.1.call-start
  8.7 0.1 shift_right_arithmetic.28
  8.8 0.1 shift_right_arithmetic.30
  8.9 1.1 shift_right_arithmetic.25
  10.0 0.2 shift_right_arithmetic.26
  10.2 44.1 %all-gather.4.cloned.1.call-done = bf16[2,80,4096]{2,1,0:T(8,128)(2,1)} async-done(((bf16[2,80,512]{2,1,0:T(8,128)(2,1)}), bf16[2,80,4096]{2,1,0:T(8,128)(2,1)}) %all-gather.4.cloned.1.call-update) | async-done | bytes 1310736 | tf_op jit(solution)/shard_map/all_gather | solution.py:25
  54.3 12.8 %fusion.4 = (bf16[160,2048]{1,0:T(8,128)(2,1)S(1)}, bf16[160,2048]{1,0:T(8,128)(2,1)S(1)}, bf16[160,2048]{1,0:T(8,128)(2,1)S(1)}) fusion(s32[160,2048]{1,0:T(8,128)S(1)} %shift_right_arithmetic.26, bf16[2,80,2048]{2,1,0:T(8,128)(2,1)} %param.10, s32[160]{0:T(256)S(1)} %shift_right_arithmetic.30, bf16[2,80,2048]{2,1,0:T(8,128)(2,1)} %param.9, ...), kind=kOutput, calls=%fused_computation.10 | convolution fusion | flops 2692546560 | bytes 22676096 | tf_op jit(solution)/shard_map/dot_general | solution.py:34
  67.1 1.4 pad_maximum_fusion
  68.5 0.0 all-gather.6.cloned.1.call-update
  68.5 27.8 %all-gather.8.cloned.1.call-done = bf16[2,80,4096]{2,1,0:T(8,128)(2,1)} async-done(((bf16[2,80,512]{2,1,0:T(8,128)(2,1)}), bf16[2,80,4096]{2,1,0:T(8,128)(2,1)}) %all-gather.8.cloned.1.call-update) | async-done | bytes 1310736 | tf_op jit(solution)/shard_map/all_gather | solution.py:26
  96.3 3.2 %all_to_all.27 = bf16[160,4,1024]{2,1,0:T(4,128)(2,1)S(1)} reshape(bf16[2,80,4096]{2,1,0:T(8,128)(2,1)} %all-gather.8.cloned.1.call-done) | data formatting | bytes 2621440 | tf_op jit(solution)/shard_map/all_to_all | solution.py:40
  99.5 1.4 copy.12
  101.0 0.0 copy-start
  101.0 4.5 %all-to-all-start.1 = ((bf16[160,4,1024]{2,0,1:T(8,128)(2,1)}), bf16[160,4,1024]{2,0,1:T(8,128)(2,1)}, u32[]{:S(2)}, u32[]{:S(2)}) async-start(bf16[160,4,1024]{2,0,1:T(8,128)(2,1)} %copy.12), calls=%async_computation.1 | async-start | bytes 2621440 | tf_op jit(solution)/shard_map/all_to_all | solution.py:40
  105.5 0.0 copy-done
  105.5 1.0 all_to_all.24
  106.5 1.5 copy.11
  108.0 29.0 %all-to-all-done.1 = bf16[160,4,1024]{2,0,1:T(8,128)(2,1)} async-done(((bf16[160,4,1024]{2,0,1:T(8,128)(2,1)}), bf16[160,4,1024]{2,0,1:T(8,128)(2,1)}, u32[]{:S(2)}, u32[]{:S(2)}) %all-to-all-start.1) | async-done | bytes 1310752 | tf_op jit(solution)/shard_map/all_to_all | solution.py:40
  137.0 3.7 %all-to-all-start = ((bf16[160,4,1024]{2,0,1:T(8,128)(2,1)}), bf16[160,4,1024]{2,0,1:T(8,128)(2,1)S(1)}, u32[]{:S(2)}, u32[]{:S(2)}) async-start(bf16[160,4,1024]{2,0,1:T(8,128)(2,1)} %copy.11), calls=%async_computation | async-start | bytes 2621440 | tf_op jit(solution)/shard_map/all_to_all | solution.py:41
  140.8 39.4 %all-gather.6.cloned.1.call-done = bf16[640,6144]{1,0:T(8,128)(2,1)} async-done(((bf16[160,6144]{1,0:T(8,128)(2,1)}), bf16[640,6144]{1,0:T(8,128)(2,1)}) %all-gather.6.cloned.1.call-update) | async-done | bytes 7864336 | tf_op jit(solution)/shard_map/all_gather | solution.py:44
  180.2 19.0 %convert_reduce_fusion = bf16[4096,1024]{1,0:T(8,128)(2,1)} fusion(bf16[4,160,6144]{2,1,0:T(8,128)(2,1)} %bitcast.21, bf16[160,4,1024]{2,0,1:T(8,128)(2,1)} %all-to-all-done.1), kind=kOutput, calls=%fused_computation | convolution fusion | flops 5398069248 | bytes 14942208 | tf_op jit(solution)/shard_map/grd,grf->gdf/dot_general | solution.py:50
  199.2 6.0 %fusion.8 = (bf16[1024,2048]{0,1:T(8,128)(2,1)}, bf16[1024,2048]{0,1:T(8,128)(2,1)}) fusion(bf16[1024,4096]{0,1:T(8,128)(2,1)} %bitcast.19), kind=kLoop, calls=%fused_computation.16 | loop fusion | bytes 16777216 | tf_op jit(solution)/shard_map/slice | solution.py:66
  205.2 6.4 %copy.14 = bf16[1024,2048]{1,0:T(8,128)(2,1)} copy(bf16[1024,2048]{0,1:T(8,128)(2,1)} %get-tuple-element.6) | data formatting | bytes 8388608
  211.6 6.4 %copy.13 = bf16[1024,2048]{1,0:T(8,128)(2,1)} copy(bf16[1024,2048]{0,1:T(8,128)(2,1)} %get-tuple-element.7) | data formatting | bytes 8388608
  218.0 0.0 all-to-all-done
  218.0 9.6 %convert_reduce_fusion.1 = bf16[2048,1024]{1,0:T(8,128)(2,1)} fusion(bf16[4,160,6144]{2,1,0:T(8,128)(2,1)} %bitcast.22, bf16[160,4,1024]{2,0,1:T(8,128)(2,1)S(1)} %all-to-all-done), kind=kOutput, calls=%fused_computation.1 | convolution fusion | flops 2699034624 | bytes 8126464 | tf_op jit(solution)/shard_map/grf,grd->gfd/dot_general | solution.py:56
  (3 shorter events, 0.0 us)
Async XLA Ops:
  7.2 47.2 %all-gather.4.cloned.1.call-start = ((), (), s32[]{:S(2)}) async-start(), calls=%async_computation.2 | async-start | bytes 1474560 | tf_op jit(solution)/shard_map/all_gather | solution.py:25
  7.9 88.4 %all-gather.8.cloned.1.call-start = ((), (), s32[]{:S(2)}) async-start(), calls=%async_computation.4 | async-start | bytes 1474560 | tf_op jit(solution)/shard_map/all_gather | solution.py:26
  8.6 171.5 %all-gather.6.cloned.1.call-start = ((), (), s32[]{:S(2)}) async-start(), calls=%async_computation.3 | async-start | bytes 9830400 | tf_op jit(solution)/shard_map/all_gather | solution.py:44
  101.0 4.5 %copy-start = (bf16[2,80,4096]{2,1,0:T(8,128)(2,1)S(1)}, bf16[2,80,4096]{2,1,0:T(8,128)(2,1)}, u32[]{:S(2)}) copy-start(bf16[2,80,4096]{2,1,0:T(8,128)(2,1)} %all-gather.4.cloned.1.call-done) | copy-start | bytes 3932164
  101.0 36.0 %all-to-all-start.1 = ((bf16[160,4,1024]{2,0,1:T(8,128)(2,1)}), bf16[160,4,1024]{2,0,1:T(8,128)(2,1)}, u32[]{:S(2)}, u32[]{:S(2)}) async-start(bf16[160,4,1024]{2,0,1:T(8,128)(2,1)} %copy.12), calls=%async_computation.1 | async-start | bytes 2621440 | tf_op jit(solution)/shard_map/all_to_all | solution.py:40
  137.0 81.0 %all-to-all-start = ((bf16[160,4,1024]{2,0,1:T(8,128)(2,1)}), bf16[160,4,1024]{2,0,1:T(8,128)(2,1)S(1)}, u32[]{:S(2)}, u32[]{:S(2)}) async-start(bf16[160,4,1024]{2,0,1:T(8,128)(2,1)} %copy.11), calls=%async_computation | async-start | bytes 2621440 | tf_op jit(solution)/shard_map/all_to_all | solution.py:41
Sparse Core Ops, SparseCore 0:
  10.0 44.2 all-gather.3
  56.4 39.8 all-gather.7
  98.4 81.6 all-gather.5
where the time goes:
time: 235 us; the launch traced here: 234 us
  waiting for transfers between devices  142 us (60%)
  matrix products  41.4 us (18%)
  local copies, waits for them, and re-layouts  27.5 us (12%)
  between operations  13.8 us (6%)
  starting transfers between devices  8.34 us (4%)
    all_gather x1, waiting for transfers between devices, shards(): lax.all_gather(out_grad, 'tensor', axis=2, tiled=True)  44.1 us
    all_gather x1, waiting for transfers between devices, shards(): values = lax.all_gather(activations, 'dp', axis=0, tiled=True)  39.4 us
    all_to_all x1, waiting for transfers between devices, shards(): lax.all_to_all(input_all, 'dp', split_axis=1, concat_axis=0, tiled=True)  29 us
    all_gather x1, waiting for transfers between devices, shards(): lax.all_gather(layer_input, 'tensor', axis=2, tiled=True)  27.8 us
    dot_general x1, matrix products, shards(): jnp.einsum('grd,grf->gdf', inputs_3d, values_3d[:, :, :2 * hidden_width],...  19 us
    unnamed x4, local copies, waits for them, and re-layouts  12.8 us
    dot_general x1, matrix products, shards(): lax.dot_general(output_all, w_down, (((1,), (1,)), ((), ())), preferred_e...  12.8 us
    dot_general x1, matrix products, shards(): jnp.einsum('grf,grd->gfd', values_3d[:, :, 2 * hidden_width:], outputs_3d...  9.61 us
  transfers between devices with their start and end apart: 5, of which 4 were waited for; matrix products, arithmetic and copies ran while one was open for 24% of the time, Pallas kernels for 0%

commit v1 on v0

--- a/solution.py
+++ b/solution.py
@@ -22,7 +22,7 @@
     hidden_width = w_down.shape[0]
     group_rows = micro_count * out_grad.shape[1]
     grad_rows, input_rows = (
-        lax.all_gather(out_grad, "tensor", axis=2, tiled=True),
+        jnp.concatenate(lax.all_gather(out_grad, "tensor"), axis=2),
         lax.all_gather(layer_input, "tensor", axis=2, tiled=True),
     )
     output_all = grad_rows.reshape(-1, model_width)

time: 235 us -> 236 us (level)
  waiting for transfers between devices: 142 us -> 137 us
  local copies, waits for them, and re-layouts: 27.5 us -> 31 us
    all_gather x1, waiting for transfers between devices: 27.8 us -> 22.1 us  [shards(): lax.all_gather(layer_input, 'tensor', axis=2, tiled=True)]
    unnamed x4 -> x3, local copies, waits for them, and re-layouts: 12.8 us -> 14.4 us
  transfers between devices with their start and end apart: 5 -> 5, of which waited for: 4 -> 4; matrix products, arithmetic and copies ran while one was open for 24% -> 27% of each run, Pallas kernels for 0% -> 0%
where the time goes in v1:
time: 236 us; the launch traced here: 235 us
  waiting for transfers between devices  137 us (58%)
  matrix products  42.6 us (18%)
  local copies, waits for them, and re-layouts  31 us (13%)
  between operations  13.8 us (6%)
  starting transfers between devices  8.21 us (3%)
  other arithmetic  2.72 us (1%)
    all_gather x1, waiting for transfers between devices, shards(): lax.all_gather(out_grad, 'tensor')  44.5 us
    all_gather x1, waiting for transfers between devices, shards(): values = lax.all_gather(activations, 'dp', axis=0, tiled=True)  39.6 us
    all_to_all x1, waiting for transfers between devices, shards(): lax.all_to_all(input_all, 'dp', split_axis=1, concat_axis=0, tiled=True)  29.2 us
    all_gather x1, waiting for transfers between devices, shards(): lax.all_gather(layer_input, 'tensor', axis=2, tiled=True)  22.1 us
    dot_general x1, matrix products, shards(): jnp.einsum('grd,grf->gdf', inputs_3d, values_3d[:, :, :2 * hidden_width],...  19 us
    unnamed x3, local copies, waits for them, and re-layouts  14.4 us
    dot_general x1, matrix products, shards(): lax.dot_general(output_all, w_down, (((1,), (1,)), ((), ())), preferred_e...  14 us
    dot_general x1, matrix products, shards(): jnp.einsum('grf,grd->gfd', values_3d[:, :, 2 * hidden_width:], outputs_3d...  9.62 us
  transfers between devices with their start and end apart: 5, of which 4 were waited for; matrix products, arithmetic and copies ran while one was open for 27% of the time, Pallas kernels for 0%

profile of v1, /device:TPU:0, one launch (start us, length us, event | category | flops | bytes accessed | tf_op | source)
XLA Modules:
  0.0 235.1 jit_solution(9977809601328238962)
XLA Ops:
  7.2 0.0 all-gather.9.cloned.1.call-start
  7.2 0.7 all-gather.9.cloned.1.call-update
  7.9 0.0 all-gather.7.cloned.1.call-start
  7.9 0.7 all-gather.7.cloned.1.call-update
  8.6 0.0 all-gather.5.cloned.1.call-start
  8.7 0.1 shift_right_arithmetic.28
  8.8 0.1 shift_right_arithmetic.30
  8.9 1.1 shift_right_arithmetic.25
  10.0 0.2 shift_right_arithmetic.26
  10.2 44.5 %all-gather.9.cloned.1.call-done = bf16[16,80,512]{2,1,0:T(8,128)(2,1)} async-done(((bf16[2,80,512]{2,1,0:T(8,128)(2,1)}), bf16[16,80,512]{2,1,0:T(8,128)(2,1)}) %all-gather.9.cloned.1.call-update) | async-done | bytes 1310736 | tf_op jit(solution)/shard_map/all_gather | solution.py:25
  54.7 2.0 copy.20
  56.8 1.6 copy.17
  58.3 14.0 %fusion.4 = (bf16[160,2048]{1,0:T(8,128)(2,1)S(1)}, bf16[160,2048]{1,0:T(8,128)(2,1)}, bf16[160,2048]{1,0:T(8,128)(2,1)}) fusion(s32[160,2048]{1,0:T(8,128)S(1)} %shift_right_arithmetic.26, bf16[2,80,2048]{2,1,0:T(8,128)(2,1)} %param.10, s32[160]{0:T(256)S(1)} %shift_right_arithmetic.30, bf16[2,80,2048]{2,1,0:T(8,128)(2,1)} %param.9, ...), kind=kOutput, calls=%fused_computation.10 | convolution fusion | flops 2692546560 | bytes 22676096 | tf_op jit(solution)/shard_map/dot_general | solution.py:34
  72.3 2.7 %pad_maximum_fusion = bf16[160,6144]{1,0:T(8,128)(2,1)} fusion(bf16[160,2048]{1,0:T(8,128)(2,1)} %get-tuple-element.12, bf16[160,2048]{1,0:T(8,128)(2,1)} %get-tuple-element.11, bf16[160,2048]{1,0:T(8,128)(2,1)S(1)} %get-tuple-element.10), kind=kLoop, calls=%fused_computation.4 | loop fusion | flops 5898240 | bytes 3932160 | tf_op jit(solution)/shard_map/concatenate | solution.py:43
  75.0 0.0 all-gather.5.cloned.1.call-update
  75.0 22.1 %all-gather.7.cloned.1.call-done = bf16[2,80,4096]{2,1,0:T(8,128)(2,1)} async-done(((bf16[2,80,512]{2,1,0:T(8,128)(2,1)}), bf16[2,80,4096]{2,1,0:T(8,128)(2,1)}) %all-gather.7.cloned.1.call-update) | async-done | bytes 1310736 | tf_op jit(solution)/shard_map/all_gather | solution.py:26
  97.2 3.2 %all_to_all.27 = bf16[160,4,1024]{2,1,0:T(4,128)(2,1)S(1)} reshape(bf16[2,80,4096]{2,1,0:T(8,128)(2,1)} %all-gather.7.cloned.1.call-done) | data formatting | bytes 2621440 | tf_op jit(solution)/shard_map/all_to_all | solution.py:40
  100.4 1.4 copy.14
  101.9 4.3 %all-to-all-start.1 = ((bf16[160,4,1024]{2,0,1:T(8,128)(2,1)}), bf16[160,4,1024]{2,0,1:T(8,128)(2,1)}, u32[]{:S(2)}, u32[]{:S(2)}) async-start(bf16[160,4,1024]{2,0,1:T(8,128)(2,1)} %copy.14), calls=%async_computation.1 | async-start | bytes 2621440 | tf_op jit(solution)/shard_map/all_to_all | solution.py:40
  106.2 0.9 all_to_all.24
  107.1 1.5 copy.13
  108.6 29.2 %all-to-all-done.1 = bf16[160,4,1024]{2,0,1:T(8,128)(2,1)} async-done(((bf16[160,4,1024]{2,0,1:T(8,128)(2,1)}), bf16[160,4,1024]{2,0,1:T(8,128)(2,1)}, u32[]{:S(2)}, u32[]{:S(2)}) %all-to-all-start.1) | async-done | bytes 1310752 | tf_op jit(solution)/shard_map/all_to_all | solution.py:40
  137.7 3.8 %all-to-all-start = ((bf16[160,4,1024]{2,0,1:T(8,128)(2,1)}), bf16[160,4,1024]{2,0,1:T(8,128)(2,1)S(1)}, u32[]{:S(2)}, u32[]{:S(2)}) async-start(bf16[160,4,1024]{2,0,1:T(8,128)(2,1)} %copy.13), calls=%async_computation | async-start | bytes 2621440 | tf_op jit(solution)/shard_map/all_to_all | solution.py:41
  141.5 39.6 %all-gather.5.cloned.1.call-done = bf16[640,6144]{1,0:T(8,128)(2,1)} async-done(((bf16[160,6144]{1,0:T(8,128)(2,1)}), bf16[640,6144]{1,0:T(8,128)(2,1)}) %all-gather.5.cloned.1.call-update) | async-done | bytes 7864336 | tf_op jit(solution)/shard_map/all_gather | solution.py:44
  181.1 19.0 %convert_reduce_fusion = bf16[4096,1024]{1,0:T(8,128)(2,1)} fusion(bf16[4,160,6144]{2,1,0:T(8,128)(2,1)} %bitcast.32, bf16[160,4,1024]{2,0,1:T(8,128)(2,1)} %all-to-all-done.1), kind=kOutput, calls=%fused_computation | convolution fusion | flops 5398069248 | bytes 14942208 | tf_op jit(solution)/shard_map/grd,grf->gdf/dot_general | solution.py:50
  200.1 6.0 %fusion.8 = (bf16[1024,2048]{0,1:T(8,128)(2,1)}, bf16[1024,2048]{0,1:T(8,128)(2,1)}) fusion(bf16[1024,4096]{0,1:T(8,128)(2,1)} %bitcast.29), kind=kLoop, calls=%fused_computation.17 | loop fusion | bytes 16777216 | tf_op jit(solution)/shard_map/slice | solution.py:66
  206.1 6.4 %copy.16 = bf16[1024,2048]{1,0:T(8,128)(2,1)} copy(bf16[1024,2048]{0,1:T(8,128)(2,1)} %get-tuple-element.6) | data formatting | bytes 8388608
  212.5 6.4 %copy.15 = bf16[1024,2048]{1,0:T(8,128)(2,1)} copy(bf16[1024,2048]{0,1:T(8,128)(2,1)} %get-tuple-element.7) | data formatting | bytes 8388608
  218.9 0.0 all-to-all-done
  219.0 9.6 %convert_reduce_fusion.1 = bf16[2048,1024]{1,0:T(8,128)(2,1)} fusion(bf16[4,160,6144]{2,1,0:T(8,128)(2,1)} %bitcast.33, bf16[160,4,1024]{2,0,1:T(8,128)(2,1)S(1)} %all-to-all-done), kind=kOutput, calls=%fused_computation.1 | convolution fusion | flops 2699034624 | bytes 8126464 | tf_op jit(solution)/shard_map/grf,grd->gfd/dot_general | solution.py:56
  (3 shorter events, 0.0 us)
Async XLA Ops:
  7.2 47.6 %all-gather.9.cloned.1.call-start = ((), (), s32[]{:S(2)}) async-start(), calls=%async_computation.4 | async-start | bytes 1474560 | tf_op jit(solution)/shard_map/all_gather | solution.py:25
  7.9 89.3 %all-gather.7.cloned.1.call-start = ((), (), s32[]{:S(2)}) async-start(), calls=%async_computation.3 | async-start | bytes 1474560 | tf_op jit(solution)/shard_map/all_gather | solution.py:26
  8.6 172.4 %all-gather.5.cloned.1.call-start = ((), (), s32[]{:S(2)}) async-start(), calls=%async_computation.2 | async-start | bytes 9830400 | tf_op jit(solution)/shard_map/all_gather | solution.py:44
  101.9 35.9 %all-to-all-start.1 = ((bf16[160,4,1024]{2,0,1:T(8,128)(2,1)}), bf16[160,4,1024]{2,0,1:T(8,128)(2,1)}, u32[]{:S(2)}, u32[]{:S(2)}) async-start(bf16[160,4,1024]{2,0,1:T(8,128)(2,1)} %copy.14), calls=%async_computation.1 | async-start | bytes 2621440 | tf_op jit(solution)/shard_map/all_to_all | solution.py:40
  137.7 81.2 %all-to-all-start = ((bf16[160,4,1024]{2,0,1:T(8,128)(2,1)}), bf16[160,4,1024]{2,0,1:T(8,128)(2,1)S(1)}, u32[]{:S(2)}, u32[]{:S(2)}) async-start(bf16[160,4,1024]{2,0,1:T(8,128)(2,1)} %copy.13), calls=%async_computation | async-start | bytes 2621440 | tf_op jit(solution)/shard_map/all_to_all | solution.py:41
Sparse Core Ops, SparseCore 0:
  10.2 44.5 all-gather.8
  56.8 40.3 all-gather.6
  99.3 81.6 all-gather.4
